TPU v7x, 32 devices: a whole 2x2x4 slice. The times are simulated.
32 devices in a mesh: grp: 2 (over y), fib: 4 (over z), wav: 2 (over x), arm: 2 (over core).
Axes of the slice: x: 2, y: 2, z: 4, core: 2. Of those that a mesh axis runs over, the one named last changes fastest.
Arguments:
- spectra: bfloat16 [32, 2, 2, 128, 256], P(('grp', 'fib'), 'arm', None, None, 'wav'), parts along dimension 0, as said below
- bands: bfloat16 [32, 2, 11, 128, 256], P(('grp', 'fib'), 'arm', None, None, 'wav'), parts along dimension 0, may hold values from 0 to 0.29882812
- coverage: int32 [32, 128], P(('grp', 'fib')), parts along dimension 0, may hold values from 0 to 1, as said below
Outputs:
- flux_coadd: float32 [2, 256, 256], P('arm', ('grp', 'fib'), 'wav'), parts along dimension 1
- ivar_coadd: float32 [2, 256, 256], P('arm', ('grp', 'fib'), 'wav'), parts along dimension 1
- res_coadd: float32 [2, 11, 256, 256], P('arm', None, ('grp', 'fib'), 'wav'), parts along dimension 2
- model: float32 [2, 256, 256], P('arm', ('grp', 'fib'), 'wav'), parts along dimension 1
There are 2 independent parts, one for each index of `grp`. A program takes and returns all parts, laid end to end along the dimension named above; each array names one. Nothing has to cross between parts.
Inputs may be any that keep to these rules, and one draw needn't show every extreme that they name: `spectra`: channel 1 (inverse variance) lies between 0.25 and 4. `coverage`: every fiber is observed by at least one exposure.
All inputs are finite; a program needn't handle non-finite values.
Results may differ from a plain program's by a relative error of at most 0.0003.
Values may be sent and summed in bfloat16 or wider, within the bound.
A program may use at most 64 MiB of HBM per device.

v0:
```python
import functools

import jax
import jax.numpy as jnp
from jax import lax
from jax.experimental import pallas as pl
from jax.experimental.pallas import tpu as pltpu
from jax.sharding import PartitionSpec as P

MESH = pl.DeviceIdType.MESH
HALF = 5
UNIT = 512.0
TOP = 32767.0
TINY = 1e-30
ROWS = 16


def kernel(n_fib, n_wav, spec_hbm, bands_hbm, cov_hbm, flux_out, ivar_out, res_out, model_out,
           spec, bands, cov, weight, flux_send, ivar_send, scale_send, band_send,
           flux_recv, ivar_recv, scale_recv, band_recv, own_band, flux_full, side, rolled,
           load_sem, send_sem, recv_sem, side_send_sem, side_recv_sem):
    f32 = jnp.float32
    me = lax.axis_index("fib")
    w_me = lax.axis_index("wav")
    right, left = lax.rem(w_me + 1, n_wav), lax.rem(w_me + n_wav - 1, n_wav)
    exposures, n_bands, fibers, width = bands.shape
    share = fibers // n_fib

    cov_load = pltpu.make_async_copy(cov_hbm, cov, load_sem.at[0])
    spec_load = pltpu.make_async_copy(spec_hbm, spec, load_sem.at[1])
    band_load = pltpu.make_async_copy(bands_hbm, bands, load_sem.at[2])
    cov_load.start()
    spec_load.start()
    band_load.start()

    def peer(t):
        low = n_fib - 1 - t
        low = jnp.where(low <= me, low - 1, low)
        high = jnp.where(t >= me, t + 1, t)
        return jnp.where(2 * me < n_fib, low, high)

    barrier = pltpu.get_barrier_semaphore()

    def greet(t, c):
        pl.semaphore_signal(barrier, inc=1, device_id={"fib": peer(t)}, device_id_type=MESH)
        return c

    lax.fori_loop(0, n_fib - 1, greet, 0)
    pl.semaphore_signal(barrier, inc=1, device_id={"wav": right}, device_id_type=MESH)
    pl.semaphore_signal(barrier, inc=1, device_id={"wav": left}, device_id_type=MESH)

    cov_load.wait()
    spec_load.wait()

    seen = cov[...].astype(f32)
    for e in range(exposures):
        column = jnp.transpose(jnp.broadcast_to(seen[e : e + 1, :], (width, fibers)))
        weight[e] = spec[e, 1].astype(f32) * column

    def head(d):
        rows = pl.ds(pl.multiple_of(d * share, share), share)
        w = [weight[e, rows, :] for e in range(exposures)]
        ivar = w[0]
        flux = w[0] * spec[0, 0, rows, :].astype(f32)
        for e in range(1, exposures):
            ivar += w[e]
            flux += w[e] * spec[e, 0, rows, :].astype(f32)
        return ivar, flux

    def copies(kind, t):
        src, dst = ((flux_send, flux_recv), (ivar_send, ivar_recv),
                    (scale_send, scale_recv), (band_send, band_recv))[kind]
        d = peer(t)
        return pltpu.make_async_remote_copy(
            src_ref=src.at[d], dst_ref=dst.at[me], send_sem=send_sem.at[kind, d],
            recv_sem=recv_sem.at[kind, me], device_id={"fib": d}, device_id_type=MESH)

    def arrival(kind, t):
        src, dst = ((flux_send, flux_recv), (ivar_send, ivar_recv),
                    (scale_send, scale_recv), (band_send, band_recv))[kind]
        d = peer(t)
        return pltpu.make_async_remote_copy(
            src_ref=src.at[d], dst_ref=dst.at[d], send_sem=send_sem.at[kind, d],
            recv_sem=recv_sem.at[kind, d], device_id={"fib": d}, device_id_type=MESH)

    def make_head(t, c):
        d = peer(t)
        ivar, flux = head(d)
        flux_send[d] = flux
        ivar_send[d] = (ivar * UNIT).astype(jnp.int32).astype(jnp.int16)
        return c

    lax.fori_loop(0, n_fib - 1, make_head, 0)
    pl.semaphore_wait(barrier, n_fib + 1)

    def send_head(t, c):
        copies(0, t).start()
        copies(1, t).start()
        return c

    lax.fori_loop(0, n_fib - 1, send_head, 0)
    band_load.wait()

    def sums(d, j):
        rows = pl.ds(pl.multiple_of(d * share + j * ROWS, ROWS), ROWS)
        w = [weight[e, rows, :] for e in range(exposures)]
        out = []
        for b in range(n_bands):
            total = w[0] * bands[0, b, rows, :].astype(f32)
            for e in range(1, exposures):
                total += w[e] * bands[e, b, rows, :].astype(f32)
            out.append(total)
        return out

    def make_bands(t, c):
        d = peer(t)
        for j in range(share // ROWS):
            piece = pl.ds(j * ROWS, ROWS)
            total = sums(d, j)
            top = functools.reduce(jnp.maximum, total)
            scale = (jnp.maximum(top, TINY) * 1.01).astype(jnp.bfloat16)
            scale_send[d, piece, :] = scale
            factor = TOP / scale.astype(f32)
            for b in range(n_bands):
                band_send[d, b, piece, :] = (total[b] * factor + 0.5).astype(jnp.int32).astype(jnp.int16)
        copies(2, t).start()
        copies(3, t).start()
        return c

    lax.fori_loop(0, n_fib - 1, make_bands, 0)

    for j in range(share // ROWS):
        total = sums(me, j)
        for b in range(n_bands):
            own_band[b, pl.ds(j * ROWS, ROWS), :] = total[b]
    ivar, flux = head(me)

    def add_head(t, carry):
        ivar, flux = carry
        d = peer(n_fib - 2 - t)
        arrival(0, n_fib - 2 - t).wait_recv()
        arrival(1, n_fib - 2 - t).wait_recv()
        return ivar + ivar_recv[d].astype(f32) * (1.0 / UNIT), flux + flux_recv[d]

    ivar, flux = lax.fori_loop(0, n_fib - 1, add_head, (ivar, flux))
    inverse = 1.0 / ivar
    coadd = flux / ivar
    ivar_out[...] = ivar[None]
    flux_out[...] = coadd[None]
    flux_full[...] = coadd
    to_right = pltpu.make_async_remote_copy(
        src_ref=flux_full, dst_ref=side.at[0], send_sem=side_send_sem.at[0], recv_sem=side_recv_sem.at[0],
        device_id={"wav": right}, device_id_type=MESH)
    to_left = pltpu.make_async_remote_copy(
        src_ref=flux_full, dst_ref=side.at[1], send_sem=side_send_sem.at[1], recv_sem=side_recv_sem.at[1],
        device_id={"wav": left}, device_id_type=MESH)
    to_right.start()
    to_left.start()
    to_right.wait_recv()
    to_left.wait_recv()
    before = jnp.where(w_me == 0, 0.0, side[0])
    after = jnp.where(w_me == n_wav - 1, 0.0, side[1])
    lane = lax.broadcasted_iota(jnp.int32, (share, width), 1)
    for b in range(n_bands):
        shift = b - HALF
        if shift == 0:
            rolled[b] = coadd
        elif shift > 0:
            rolled[b] = pltpu.roll(jnp.where(lane >= shift, coadd, after), width - shift, 1)
        else:
            rolled[b] = pltpu.roll(jnp.where(lane < width + shift, coadd, before), -shift, 1)

    def add_bands(t, c):
        d = peer(n_fib - 2 - t)
        arrival(2, n_fib - 2 - t).wait_recv()
        arrival(3, n_fib - 2 - t).wait_recv()
        scale = scale_recv[d].astype(f32) * (1.0 / TOP)
        for b in range(n_bands):
            own_band[b] += band_recv[d, b].astype(f32) * scale
        return c

    lax.fori_loop(0, n_fib - 1, add_bands, 0)
    model = None
    for b in range(n_bands):
        res = own_band[b] * inverse
        res_out[0, b] = res
        term = res * rolled[b]
        model = term if model is None else model + term
    model_out[...] = model[None]

    def finish(t, c):
        for kind in range(4):
            copies(kind, t).wait_send()
        return c

    lax.fori_loop(0, n_fib - 1, finish, 0)
    to_right.wait_send()
    to_left.wait_send()


def write_out(*refs):
    half = len(refs) // 2
    sem = refs[-1]
    loads = [pltpu.make_async_copy(refs[i], refs[half + i], sem.at[i]) for i in range(half)]
    for copy in loads:
        copy.start()
    for copy in loads:
        copy.wait()


def local(n_fib, n_wav, spectra, bands, coverage):
    spectra, bands = spectra[:, 0], bands[:, 0]
    exposures, n_bands, fibers, width = bands.shape
    share = fibers // n_fib
    f32, i16, bf16 = jnp.float32, jnp.int16, jnp.bfloat16
    plane = jax.ShapeDtypeStruct((1, share, width), f32)
    vmem = pltpu.VMEM
    sem = pltpu.SemaphoreType.DMA
    shapes = (plane, plane, jax.ShapeDtypeStruct((1, n_bands, share, width), f32), plane)
    parts = pl.pallas_call(
        functools.partial(kernel, n_fib, n_wav),
        out_shape=tuple(vmem(x.shape, f32) for x in shapes),
        in_specs=[pl.BlockSpec(memory_space=pl.ANY)] * 3,
        out_specs=[pl.BlockSpec(memory_space=pltpu.VMEM)] * 4,
        scratch_shapes=[
            vmem(spectra.shape, bf16),
            vmem(bands.shape, bf16),
            vmem(coverage.shape, jnp.int32),
            vmem((exposures, fibers, width), f32),
            vmem((n_fib, share, width), f32),
            vmem((n_fib, share, width), i16),
            vmem((n_fib, share, width), bf16),
            vmem((n_fib, n_bands, share, width), i16),
            vmem((n_fib, share, width), f32),
            vmem((n_fib, share, width), i16),
            vmem((n_fib, share, width), bf16),
            vmem((n_fib, n_bands, share, width), i16),
            vmem((n_bands, share, width), f32),
            vmem((share, width), f32),
            vmem((2, share, width), f32),
            vmem((n_bands, share, width), f32),
            sem((3,)),
            sem((4, n_fib)),
            sem((4, n_fib)),
            sem((2,)),
            sem((2,)),
        ],
        compiler_params=pltpu.CompilerParams(collective_id=0, has_side_effects=True),
        name="coadd",
    )(spectra, bands, coverage)
    return pl.pallas_call(
        write_out,
        out_shape=shapes,
        in_specs=[pl.BlockSpec(memory_space=pltpu.VMEM)] * 4,
        out_specs=[pl.BlockSpec(memory_space=pl.ANY)] * 4,
        scratch_shapes=[sem((4,))],
        compiler_params=pltpu.CompilerParams(vmem_limit_bytes=4 * 2**20),
        name="write_out",
    )(*parts)


def solution(mesh):
    sizes = dict(mesh.shape)
    return jax.shard_map(
        functools.partial(local, sizes["fib"], sizes["wav"]),
        mesh=mesh,
        in_specs=(
            P(("grp", "fib"), "arm", None, None, "wav"),
            P(("grp", "fib"), "arm", None, None, "wav"),
            P(("grp", "fib"), None),
        ),
        out_specs=(
            P("arm", ("grp", "fib"), "wav"),
            P("arm", ("grp", "fib"), "wav"),
            P("arm", None, ("grp", "fib"), "wav"),
            P("arm", ("grp", "fib"), "wav"),
        ),
        check_vma=False,
    )
```

profile of v0, /device:TPU:0, one launch (start us, length us, event | category | flops | bytes accessed | tf_op | source)
XLA Modules:
  0.0 17.5 jit_solution(13153677175359605012)
XLA Ops:
  0.6 16.1 %coadd.1 = (f32[1,32,128]{2,1,0:T(8,128)S(1)}, f32[1,32,128]{2,1,0:T(8,128)S(1)}, f32[1,11,32,128]{3,2,1,0:T(8,128)S(1)}, f32[1,32,128]{2,1,0:T(8,128)S(1)}) custom-call(bf16[4,2,128,128]{3,2,1,0:T(8,128)(2,1)} %bitcast.3, bf16[4,11,128,128]{3,2,1,0:T(8,128)(2,1)} %bitcast.2, s32[4,128]{1,0:T(4,128)} %cov_hbm.1), custom_call_target="tpu_custom_call" | custom-call | tf_op jit(solution)/shard_map/coadd/pallas_call | solution.py:220
  16.7 0.7 %write_out.1 = (f32[1,32,128]{2,1,0:T(8,128)}, f32[1,32,128]{2,1,0:T(8,128)}, f32[1,11,32,128]{3,2,1,0:T(8,128)}, f32[1,32,128]{2,1,0:T(8,128)}) custom-call(f32[1,32,128]{2,1,0:T(8,128)S(1)} %get-tuple-element.8.refs_0_, f32[1,32,128]{2,1,0:T(8,128)S(1)} %get-tuple-element.9.refs_1_, f32[1,11,32,128]{3,2,1,0:T(8,128)S(1)} %get-tuple-element.10.refs_2_, ...), custom_call_target="tpu_custom_call" | custom-call | tf_op jit(solution)/shard_map/write_out/pallas_call | solution.py:251
where the time goes:
time: 17.6 us; the launch traced here: 17.5 us
  Pallas kernels  16.8 us (95%)
  between operations  0.64 us (4%)
    pallas_call x1, Pallas kernels, local(): pl.pallas_call(functools.partial(kernel, n_fib, n_wav), out_shape=tuple((...  16.1 us
    pallas_call x1, Pallas kernels, local(): pl.pallas_call(write_out, out_shape=shapes, in_specs=[pl.BlockSpec(memory...  0.72 us

commit v1 on v0

--- a/solution.py
+++ b/solution.py
@@ -17,8 +17,8 @@
 
 def kernel(n_fib, n_wav, spec_hbm, bands_hbm, cov_hbm, flux_out, ivar_out, res_out, model_out,
            spec, bands, cov, weight, flux_send, ivar_send, scale_send, band_send,
-           flux_recv, ivar_recv, scale_recv, band_recv, own_band, flux_full, side, rolled,
-           load_sem, send_sem, recv_sem, side_send_sem, side_recv_sem):
+           flux_recv, ivar_recv, scale_recv, band_recv, own_band, held, flux_full, side, rolled,
+           load_sem, head_send_sem, head_recv_sem, send_sem, recv_sem, side_send_sem, side_recv_sem):
     f32 = jnp.float32
     me = lax.axis_index("fib")
     w_me = lax.axis_index("wav")
@@ -56,6 +56,12 @@
     for e in range(exposures):
         column = jnp.transpose(jnp.broadcast_to(seen[e : e + 1, :], (width, fibers)))
         weight[e] = spec[e, 1].astype(f32) * column
+
+    pieces = share // ROWS
+    is_end = (me == 0) | (me == n_fib - 1)
+    is_relay = (me == 1) | (me == n_fib - 2)
+    relay = jnp.where(me == 0, 1, n_fib - 2)
+    far = jnp.where(me == 1, n_fib - 1, 0)
 
     def head(d):
         rows = pl.ds(pl.multiple_of(d * share, share), share)
@@ -67,21 +73,25 @@
             flux += w[e] * spec[e, 0, rows, :].astype(f32)
         return ivar, flux
 
-    def copies(kind, t):
-        src, dst = ((flux_send, flux_recv), (ivar_send, ivar_recv),
-                    (scale_send, scale_recv), (band_send, band_recv))[kind]
-        d = peer(t)
-        return pltpu.make_async_remote_copy(
-            src_ref=src.at[d], dst_ref=dst.at[me], send_sem=send_sem.at[kind, d],
-            recv_sem=recv_sem.at[kind, me], device_id={"fib": d}, device_id_type=MESH)
-
-    def arrival(kind, t):
-        src, dst = ((flux_send, flux_recv), (ivar_send, ivar_recv),
-                    (scale_send, scale_recv), (band_send, band_recv))[kind]
-        d = peer(t)
-        return pltpu.make_async_remote_copy(
-            src_ref=src.at[d], dst_ref=dst.at[d], send_sem=send_sem.at[kind, d],
-            recv_sem=recv_sem.at[kind, d], device_id={"fib": d}, device_id_type=MESH)
+    def head_copies(d, slot):
+        return [pltpu.make_async_remote_copy(
+            src_ref=src.at[d], dst_ref=dst.at[slot], send_sem=head_send_sem.at[kind, d],
+            recv_sem=head_recv_sem.at[kind, slot], device_id={"fib": d}, device_id_type=MESH)
+            for kind, (src, dst) in enumerate(((flux_send, flux_recv), (ivar_send, ivar_recv)))]
+
+    def tail_copies(d, j, to, slot):
+        return [pltpu.make_async_remote_copy(
+            src_ref=src.at[d, j], dst_ref=dst.at[slot, j], send_sem=send_sem.at[kind, d, j],
+            recv_sem=recv_sem.at[kind, slot, j], device_id={"fib": to}, device_id_type=MESH)
+            for kind, (src, dst) in enumerate(((scale_send, scale_recv), (band_send, band_recv)))]
+
+    def order(t):
+        return peer(jnp.where(is_relay, lax.rem(t + 1, n_fib - 1), t))
+
+    def send_tail(t, j):
+        d = order(t)
+        relayed = is_end & (t == 0)
+        return tail_copies(d, j, jnp.where(relayed, relay, d), jnp.where(relayed, relay, me))
 
     def make_head(t, c):
         d = peer(t)
@@ -91,14 +101,6 @@
         return c
 
     lax.fori_loop(0, n_fib - 1, make_head, 0)
-    pl.semaphore_wait(barrier, n_fib + 1)
-
-    def send_head(t, c):
-        copies(0, t).start()
-        copies(1, t).start()
-        return c
-
-    lax.fori_loop(0, n_fib - 1, send_head, 0)
     band_load.wait()
 
     def sums(d, j):
@@ -112,34 +114,69 @@
             out.append(total)
         return out
 
+    def pack(d, j, total):
+        top = functools.reduce(jnp.maximum, total)
+        scale = (jnp.maximum(top, TINY) * 1.01).astype(jnp.bfloat16)
+        scale_send[d, j] = scale
+        factor = TOP / scale.astype(f32)
+        for b in range(n_bands):
+            band_send[d, j, b] = (total[b] * factor + 0.5).astype(jnp.int32).astype(jnp.int16)
+
+    def store(ref, j, total):
+        for b in range(n_bands):
+            ref[b, pl.ds(j * ROWS, ROWS), :] = total[b]
+
+    for j in range(pieces):
+        d = order(0)
+        pack(d, j, sums(d, j))
+
+    pl.semaphore_wait(barrier, n_fib + 1)
+
+    def send_head(t, c):
+        for copy in head_copies(peer(t), me):
+            copy.start()
+        return c
+
+    lax.fori_loop(0, n_fib - 1, send_head, 0)
+    for j in range(pieces):
+        for copy in send_tail(0, j):
+            copy.start()
+
     def make_bands(t, c):
-        d = peer(t)
-        for j in range(share // ROWS):
-            piece = pl.ds(j * ROWS, ROWS)
-            total = sums(d, j)
-            top = functools.reduce(jnp.maximum, total)
-            scale = (jnp.maximum(top, TINY) * 1.01).astype(jnp.bfloat16)
-            scale_send[d, piece, :] = scale
-            factor = TOP / scale.astype(f32)
-            for b in range(n_bands):
-                band_send[d, b, piece, :] = (total[b] * factor + 0.5).astype(jnp.int32).astype(jnp.int16)
-        copies(2, t).start()
-        copies(3, t).start()
-        return c
-
-    lax.fori_loop(0, n_fib - 1, make_bands, 0)
-
-    for j in range(share // ROWS):
-        total = sums(me, j)
-        for b in range(n_bands):
-            own_band[b, pl.ds(j * ROWS, ROWS), :] = total[b]
+        d = order(t)
+        for j in range(pieces):
+            pack(d, j, sums(d, j))
+            for copy in send_tail(t, j):
+                copy.start()
+        return c
+
+    lax.fori_loop(1, n_fib - 1 - jnp.where(is_relay, 1, 0), make_bands, 0)
+
+    @pl.when(is_relay)
+    def _():
+        for j in range(pieces):
+            store(held, j, sums(far, j))
+
+    for j in range(pieces):
+        store(own_band, j, sums(me, j))
     ivar, flux = head(me)
+
+    @pl.when(is_relay)
+    def _():
+        for j in range(pieces):
+            for copy in tail_copies(far, j, far, me):
+                copy.wait_recv()
+            scale = scale_recv[me, j].astype(f32) * (1.0 / TOP)
+            pack(far, j, [held[b, pl.ds(j * ROWS, ROWS), :] + band_recv[me, j, b].astype(f32) * scale
+                          for b in range(n_bands)])
+            for copy in tail_copies(far, j, far, me):
+                copy.start()
 
     def add_head(t, carry):
         ivar, flux = carry
         d = peer(n_fib - 2 - t)
-        arrival(0, n_fib - 2 - t).wait_recv()
-        arrival(1, n_fib - 2 - t).wait_recv()
+        for copy in head_copies(d, d):
+            copy.wait_recv()
         return ivar + ivar_recv[d].astype(f32) * (1.0 / UNIT), flux + flux_recv[d]
 
     ivar, flux = lax.fori_loop(0, n_fib - 1, add_head, (ivar, flux))
@@ -171,15 +208,16 @@
             rolled[b] = pltpu.roll(jnp.where(lane < width + shift, coadd, before), -shift, 1)
 
     def add_bands(t, c):
-        d = peer(n_fib - 2 - t)
-        arrival(2, n_fib - 2 - t).wait_recv()
-        arrival(3, n_fib - 2 - t).wait_recv()
-        scale = scale_recv[d].astype(f32) * (1.0 / TOP)
-        for b in range(n_bands):
-            own_band[b] += band_recv[d, b].astype(f32) * scale
-        return c
-
-    lax.fori_loop(0, n_fib - 1, add_bands, 0)
+        d = peer(jnp.where(is_relay, lax.rem(2 * n_fib - 4 - t, n_fib - 1), n_fib - 2 - t))
+        for j in range(pieces):
+            for copy in tail_copies(d, j, d, d):
+                copy.wait_recv()
+            scale = scale_recv[d, j].astype(f32) * (1.0 / TOP)
+            for b in range(n_bands):
+                own_band[b, pl.ds(j * ROWS, ROWS), :] += band_recv[d, j, b].astype(f32) * scale
+        return c
+
+    lax.fori_loop(0, n_fib - 1 - jnp.where(is_end, 1, 0), add_bands, 0)
     model = None
     for b in range(n_bands):
         res = own_band[b] * inverse
@@ -189,8 +227,12 @@
     model_out[...] = model[None]
 
     def finish(t, c):
-        for kind in range(4):
-            copies(kind, t).wait_send()
+        d = peer(t)
+        for copy in head_copies(d, me):
+            copy.wait_send()
+        for j in range(pieces):
+            for copy in tail_copies(d, j, d, me):
+                copy.wait_send()
         return c
 
     lax.fori_loop(0, n_fib - 1, finish, 0)
@@ -212,6 +254,7 @@
     spectra, bands = spectra[:, 0], bands[:, 0]
     exposures, n_bands, fibers, width = bands.shape
     share = fibers // n_fib
+    pieces = share // ROWS
     f32, i16, bf16 = jnp.float32, jnp.int16, jnp.bfloat16
     plane = jax.ShapeDtypeStruct((1, share, width), f32)
     vmem = pltpu.VMEM
@@ -229,19 +272,22 @@
             vmem((exposures, fibers, width), f32),
             vmem((n_fib, share, width), f32),
             vmem((n_fib, share, width), i16),
-            vmem((n_fib, share, width), bf16),
-            vmem((n_fib, n_bands, share, width), i16),
+            vmem((n_fib, pieces, ROWS, width), bf16),
+            vmem((n_fib, pieces, n_bands, ROWS, width), i16),
             vmem((n_fib, share, width), f32),
             vmem((n_fib, share, width), i16),
-            vmem((n_fib, share, width), bf16),
-            vmem((n_fib, n_bands, share, width), i16),
+            vmem((n_fib, pieces, ROWS, width), bf16),
+            vmem((n_fib, pieces, n_bands, ROWS, width), i16),
+            vmem((n_bands, share, width), f32),
             vmem((n_bands, share, width), f32),
             vmem((share, width), f32),
             vmem((2, share, width), f32),
             vmem((n_bands, share, width), f32),
             sem((3,)),
-            sem((4, n_fib)),
-            sem((4, n_fib)),
+            sem((2, n_fib)),
+            sem((2, n_fib)),
+            sem((2, n_fib, pieces)),
+            sem((2, n_fib, pieces)),
             sem((2,)),
             sem((2,)),
         ],

time: 17.6 us -> 16.9 us (0.960)
  Pallas kernels: 16.8 us -> 16.1 us
    pallas_call x1, Pallas kernels: 16.1 us -> 15.4 us  [local(): pl.pallas_call(functools.partial(kernel, n_fib, n_wav), out_shape=tuple((...]
where the time goes in v1:
time: 16.9 us; the launch traced here: 16.7 us
  Pallas kernels  16.1 us (95%)
  between operations  0.64 us (4%)
    pallas_call x1, Pallas kernels, local(): pl.pallas_call(functools.partial(kernel, n_fib, n_wav), out_shape=tuple((...  15.4 us
    pallas_call x1, Pallas kernels, local(): pl.pallas_call(write_out, out_shape=shapes, in_specs=[pl.BlockSpec(memory...  0.72 us

profile of v1, /device:TPU:0, one launch (start us, length us, event | category | flops | bytes accessed | tf_op | source)
XLA Modules:
  0.0 16.7 jit_solution(5558798194604483984)
XLA Ops:
  0.6 15.4 %coadd.1 = (f32[1,32,128]{2,1,0:T(8,128)S(1)}, f32[1,32,128]{2,1,0:T(8,128)S(1)}, f32[1,11,32,128]{3,2,1,0:T(8,128)S(1)}, f32[1,32,128]{2,1,0:T(8,128)S(1)}) custom-call(bf16[4,2,128,128]{3,2,1,0:T(8,128)(2,1)} %bitcast.3, bf16[4,11,128,128]{3,2,1,0:T(8,128)(2,1)} %bitcast.2, s32[4,128]{1,0:T(4,128)} %cov_hbm.1), custom_call_target="tpu_custom_call" | custom-call | tf_op jit(solution)/shard_map/coadd/pallas_call | solution.py:263
  16.0 0.7 %write_out.1 = (f32[1,32,128]{2,1,0:T(8,128)}, f32[1,32,128]{2,1,0:T(8,128)}, f32[1,11,32,128]{3,2,1,0:T(8,128)}, f32[1,32,128]{2,1,0:T(8,128)}) custom-call(f32[1,32,128]{2,1,0:T(8,128)S(1)} %get-tuple-element.8.refs_0_, f32[1,32,128]{2,1,0:T(8,128)S(1)} %get-tuple-element.9.refs_1_, f32[1,11,32,128]{3,2,1,0:T(8,128)S(1)} %get-tuple-element.10.refs_2_, ...), custom_call_target="tpu_custom_call" | custom-call | tf_op jit(solution)/shard_map/write_out/pallas_call | solution.py:297

commit v2 on v1

--- a/solution.py
+++ b/solution.py
@@ -86,7 +86,8 @@
             for kind, (src, dst) in enumerate(((scale_send, scale_recv), (band_send, band_recv)))]
 
     def order(t):
-        return peer(jnp.where(is_relay, lax.rem(t + 1, n_fib - 1), t))
+        turned = jnp.where(t == 0, 0, n_fib - 1 - t)
+        return peer(jnp.where(is_relay, lax.rem(t + 1, n_fib - 1), jnp.where(is_end, turned, t)))
 
     def send_tail(t, j):
         d = order(t)
@@ -137,10 +138,21 @@
             copy.start()
         return c
 
+    def send_first():
+        for j in range(pieces):
+            for copy in send_tail(0, j):
+                copy.start()
+
+    @pl.when(is_end)
+    def _():
+        send_first()
+
     lax.fori_loop(0, n_fib - 1, send_head, 0)
-    for j in range(pieces):
-        for copy in send_tail(0, j):
-            copy.start()
+
+    @pl.when(jnp.logical_not(is_end))
+    def _():
+        send_first()
+
 
     def make_bands(t, c):
         d = order(t)

time: 16.9 us -> 16.5 us (0.976)
  Pallas kernels: 16.1 us -> 15.7 us
    pallas_call x1, Pallas kernels: 15.4 us -> 15 us  [local(): pl.pallas_call(functools.partial(kernel, n_fib, n_wav), out_shape=tuple((...]
where the time goes in v2:
time: 16.5 us; the launch traced here: 16.4 us
  Pallas kernels  15.7 us (95%)
  between operations  0.64 us (4%)
    pallas_call x1, Pallas kernels, local(): pl.pallas_call(functools.partial(kernel, n_fib, n_wav), out_shape=tuple((...  15 us
    pallas_call x1, Pallas kernels, local(): pl.pallas_call(write_out, out_shape=shapes, in_specs=[pl.BlockSpec(memory...  0.72 us

profile of v2, /device:TPU:0, one launch (start us, length us, event | category | flops | bytes accessed | tf_op | source)
XLA Modules:
  0.0 16.4 jit_solution(5031883618438838732)
XLA Ops:
  0.6 15.0 %coadd.1 = (f32[1,32,128]{2,1,0:T(8,128)S(1)}, f32[1,32,128]{2,1,0:T(8,128)S(1)}, f32[1,11,32,128]{3,2,1,0:T(8,128)S(1)}, f32[1,32,128]{2,1,0:T(8,128)S(1)}) custom-call(bf16[4,2,128,128]{3,2,1,0:T(8,128)(2,1)} %bitcast.3, bf16[4,11,128,128]{3,2,1,0:T(8,128)(2,1)} %bitcast.2, s32[4,128]{1,0:T(4,128)} %cov_hbm.1), custom_call_target="tpu_custom_call" | custom-call | tf_op jit(solution)/shard_map/coadd/pallas_call | solution.py:275
  15.6 0.7 %write_out.1 = (f32[1,32,128]{2,1,0:T(8,128)}, f32[1,32,128]{2,1,0:T(8,128)}, f32[1,11,32,128]{3,2,1,0:T(8,128)}, f32[1,32,128]{2,1,0:T(8,128)}) custom-call(f32[1,32,128]{2,1,0:T(8,128)S(1)} %get-tuple-element.8.refs_0_, f32[1,32,128]{2,1,0:T(8,128)S(1)} %get-tuple-element.9.refs_1_, f32[1,11,32,128]{3,2,1,0:T(8,128)S(1)} %get-tuple-element.10.refs_2_, ...), custom_call_target="tpu_custom_call" | custom-call | tf_op jit(solution)/shard_map/write_out/pallas_call | solution.py:309
